TPU v7x, 256 devices: a whole 4x4x8 slice. The times are simulated.
256 devices in a mesh: dp: 32 (over x, z_lo, core), head: 8 (over y, z_hi).
Axes of the slice: x: 4, y: 4, z: 8 (z_hi: 2, z_lo: 4; z = z_hi * 4 + z_lo), core: 2. Of those that a mesh axis runs over, the one named last changes fastest.
Arguments:
- frames_in: bfloat16 [32, 8, 320, 640], P('dp', 'head'), may hold values from -6 to 6
- ln1_gain: float32 [1280], replicated, may hold values from 0.25 to 1.75
- ln1_bias: float32 [1280], replicated, may hold values from -3 to 3
- qkv_weight: bfloat16 [1280, 3, 1024], P('dp', None, 'head'), may hold values from -0.1875 to 0.1875
- qv_bias: float32 [2, 1024], P(None, 'head'), may hold values from -3 to 3
- out_weight: bfloat16 [1024, 1280], P(('head', 'dp')), may hold values from -0.1875 to 0.1875
- out_bias: float32 [1280], P('head'), may hold values from -3 to 3
- ln2_gain: float32 [1280], replicated, may hold values from 0.25 to 1.75
- ln2_bias: float32 [1280], replicated, may hold values from -3 to 3
- fc1_weight: bfloat16 [1280, 5120], P('dp', 'head'), may hold values from -0.15625 to 0.15625
- fc1_bias: float32 [5120], P('head'), may hold values from -3 to 3
- fc2_weight: bfloat16 [5120, 1280], P(('head', 'dp')), may hold values from -0.078125 to 0.078125
- fc2_bias: float32 [1280], P('head'), may hold values from -3 to 3
- server_of_clip: int32 [32], replicated, may hold values from 0 to 7
Outputs:
- encoded: bfloat16 [32, 8, 320, 640], P('dp', 'head')
All inputs are finite; a program needn't handle non-finite values.
Results may differ from a plain program's by a relative error of at most 0.014.
Values may be sent and summed in bfloat16 or wider, within the bound.
No kernel may reach another device: no remote copies, remote signals or barrier semaphores. Data moves between devices by JAX's collectives and lax.ppermute only.
A program may use at most 64 MiB of HBM per device.

v0:
```python
import jax
import jax.numpy as jnp
from jax import lax
from jax.sharding import Mesh
from jax.sharding import PartitionSpec as P

HDIM = 64
HEAD = ("head_0", "head_1")
HEAD_DP = ("head_0", "head_1", "dp")
epsilon = 1e-05


def laid_out(blocks, dim):
    dims = list(blocks.shape[1:])
    dims[dim] *= blocks.shape[0]
    return jnp.moveaxis(blocks, 0, dim).reshape(dims)


def sent_to_all(value, axis):
    copies = jnp.broadcast_to(value, (lax.axis_size(axis), *value.shape))
    return lax.all_to_all(copies, axis, split_axis=0, concat_axis=0, tiled=True)


def gather_directly(value, axis, dim):
    return laid_out(sent_to_all(value, axis), dim)


def own_rows(terms, axes):
    total = terms.astype(jnp.bfloat16)
    for axis in axes:
        total = lax.psum_scatter(total, axis, scatter_dimension=0, tiled=True)
    return total.astype(jnp.float32)


def layer_norm(matrix, gain_row, shift_row):
    floats = matrix.astype(jnp.float32)
    center = jnp.mean(floats, axis=-1, keepdims=True)
    spread = jnp.mean(jnp.square(floats - center), axis=-1, keepdims=True)
    return ((floats - center) * lax.rsqrt(spread + epsilon) * gain_row + shift_row).astype(
        jnp.bfloat16
    )


def normalize(residual_in, gain_row, shift_row):
    whole_rows = lax.all_gather(residual_in, HEAD, axis=1, tiled=True)
    return layer_norm(whole_rows, gain_row, shift_row)


def attend(queries, key_rows, value_rows):

    def single(triple):
        query_head, key_head, value_head = triple
        scores = jnp.dot(query_head, key_head.T, preferred_element_type=jnp.float32)
        maxima = jnp.max(scores, axis=-1, keepdims=True)
        weights = jnp.exp(scores - maxima)
        probability = (weights / jnp.sum(weights, axis=-1, keepdims=True)).astype(jnp.bfloat16)
        return jnp.dot(probability, value_head, preferred_element_type=jnp.float32).astype(
            jnp.bfloat16
        )

    per_head = lax.map(
        single,
        (jnp.swapaxes(queries, 0, 1), jnp.swapaxes(key_rows, 0, 1), jnp.swapaxes(value_rows, 0, 1)),
    )
    return jnp.swapaxes(per_head, 0, 1).reshape(queries.shape[0], -1)


def slot_order(server_list):
    clip_count = server_list.shape[0]
    indices = jnp.arange(clip_count, dtype=jnp.int32)
    earlier = (server_list[None, :] < server_list[:, None]) | (
        server_list[None, :] == server_list[:, None]
    ) & (indices[None, :] < indices[:, None])
    slot_of = jnp.sum(earlier.astype(jnp.int32), axis=1)
    return jnp.sum(jnp.where(slot_of[None, :] == indices[:, None], indices[None, :], 0), axis=1)


def regroup(block_rows, clip_order):
    group_size = lax.axis_size("dp")
    piece_rows = block_rows.reshape(group_size, -1)
    shuffled = lax.all_to_all(piece_rows, "dp", split_axis=0, concat_axis=0, tiled=True)
    picked = jnp.take(shuffled, clip_order, axis=0)
    returned = lax.all_to_all(picked, "dp", split_axis=0, concat_axis=0, tiled=True)
    return returned.reshape(block_rows.shape)


def block_term(operand, weight_rows, row_count, frame_count, local_width):
    blocks = row_count // frame_count
    product = jnp.dot(operand, weight_rows, preferred_element_type=jnp.float32)
    return (
        product.reshape(frame_count, blocks, local_width)
        .transpose(1, 0, 2)
        .reshape(blocks * frame_count, local_width)
    )


def on_device(
    frames_in,
    ln1_gain,
    ln1_bias,
    qkv_weight,
    qv_bias,
    out_weight,
    out_bias,
    ln2_gain,
    ln2_bias,
    fc1_weight,
    fc1_bias,
    fc2_weight,
    fc2_bias,
    server_of_clip,
):
    clip_order = slot_order(server_of_clip)
    group_rows = frames_in.shape[2]
    local_width = frames_in.shape[3] // 4
    frame_count = group_rows * 4
    residual_in = frames_in[0, 0].reshape(frame_count, local_width)
    residual_in = regroup(residual_in, clip_order)
    head_count = lax.axis_size(HEAD)
    normed_one = normalize(residual_in, ln1_gain, ln1_bias)
    column_count = qkv_weight.shape[2]
    weight_piece = lax.all_gather(qkv_weight, "dp", axis=0, tiled=True)
    operand = normed_one
    projected = jnp.dot(
        operand, weight_piece.reshape(weight_piece.shape[0], -1), preferred_element_type=jnp.float32
    ).reshape(frame_count, 3, column_count)
    queries = (
        ((projected[:, 0] + qv_bias[0]) * HDIM ** (-0.5))
        .astype(jnp.bfloat16)
        .reshape(frame_count, -1, HDIM)
    )
    key_rows = projected[:, 1].astype(jnp.bfloat16).reshape(frame_count, -1, HDIM)
    value_rows = (projected[:, 2] + qv_bias[1]).astype(jnp.bfloat16).reshape(frame_count, -1, HDIM)
    context = attend(queries, key_rows, value_rows)
    output_rows = lax.all_gather(out_weight, "dp", axis=0, tiled=True)
    carried = residual_in.astype(jnp.float32) + out_bias
    whole_context = gather_directly(context, HEAD, 1)
    split_rows = output_rows.reshape(output_rows.shape[0], head_count, local_width)
    feature_columns = lax.all_to_all(
        split_rows, HEAD, split_axis=1, concat_axis=0, tiled=True
    ).reshape(-1, local_width)
    attended = (
        carried + jnp.dot(whole_context, feature_columns, preferred_element_type=jnp.float32)
    ).astype(jnp.bfloat16)
    normed_two = normalize(attended, ln2_gain, ln2_bias)
    operand = normed_two
    hidden_sums = jnp.dot(
        operand, gather_directly(fc1_weight, "dp", 0), preferred_element_type=jnp.float32
    )
    hidden = jax.nn.gelu(hidden_sums + fc1_bias, approximate=False).astype(jnp.bfloat16)
    down_rows = lax.all_gather(fc2_weight, "dp", axis=0, tiled=True)
    kept = attended.astype(jnp.float32) + fc2_bias
    layer_out = (
        kept
        + own_rows(
            block_term(
                hidden, down_rows, frame_count * lax.axis_size(HEAD), frame_count, local_width
            ),
            HEAD,
        )
    ).astype(jnp.bfloat16)
    return layer_out.reshape(1, 1, group_rows, 4 * local_width)


def solution(mesh):
    torus = Mesh(mesh.devices.reshape(mesh.shape["dp"], 4, 2), ("dp", "head_0", "head_1"))
    return jax.shard_map(
        on_device,
        mesh=torus,
        in_specs=(
            P("dp", HEAD, None, None),
            P(),
            P(),
            P("dp", None, HEAD),
            P(None, HEAD),
            P(HEAD_DP, None),
            P(HEAD),
            P(),
            P(),
            P("dp", HEAD),
            P(HEAD),
            P(HEAD_DP, None),
            P(HEAD),
            P(),
        ),
        out_specs=P("dp", HEAD, None, None),
        check_vma=False,
    )
```

profile of v0, /device:TPU:2, one launch (start us, length us, event | category | flops | bytes accessed | tf_op | source)
XLA Modules:
  0.0 519.4 jit_solution(1292017763583869009)
XLA Ops:
  7.4 2.4 all_to_all.38
  10.3 3.1 reduce.9
  13.4 0.9 reshape.166
  14.3 9.1 %all-to-all-start = ((bf16[32,2,3200]{2,1,0:T(2,128)(2,1)}), bf16[32,2,3200]{2,1,0:T(2,128)(2,1)S(1)}, u32[]{:S(2)}, u32[]{:S(2)}) async-start(bf16[32,2,3200]{2,1,0:T(2,128)(2,1)} %reshape.166), calls=%async_computation | async-start | bytes 819200 | tf_op jit(solution)/shard_map/all_to_all | solution.py:81
  23.7 11.2 %all-to-all-done = bf16[32,2,3200]{2,1,0:T(2,128)(2,1)S(1)} async-done(((bf16[32,2,3200]{2,1,0:T(2,128)(2,1)}), bf16[32,2,3200]{2,1,0:T(2,128)(2,1)S(1)}, u32[]{:S(2)}, u32[]{:S(2)}) %all-to-all-start) | async-done | bytes 409632 | tf_op jit(solution)/shard_map/all_to_all | solution.py:81
  35.3 0.8 gather_fusion
  36.2 0.9 reduce.10
  37.2 17.8 %all_to_all.44 = bf16[32,2,3200]{2,1,0:T(2,128)(2,1)S(1)} all-to-all(bf16[32,2,3200]{2,1,0:T(2,128)(2,1)S(1)} %reshape.168), channel_id=1, replica_groups=mesh['dp'=32,'head_0'=4,'head_1'=2] {'dp'}, dimensions={0} | all-to-all | bytes 819200 | tf_op jit(solution)/shard_map/all_to_all | solution.py:83
  55.4 2.4 reduce
  57.8 0.8 reshape.131
  58.7 1.0 copy.56
  59.7 38.8 %all-gather = bf16[32,4,1280]{2,1,0:T(4,128)(2,1)S(1)} all-gather(bf16[1,4,1280]{2,1,0:T(4,128)(2,1)S(1)} %bitcast.96), channel_id=1, replica_groups=mesh['dp'=32,'head_0'=4,'head_1'=2] {'dp'}, dimensions={0}, use_global_device_ids=true | all-gather | bytes 337920 | tf_op jit(solution)/shard_map/all_gather | solution.py:135
  98.5 0.7 reshape.135
  99.2 1.1 copy.63
  100.3 7.2 %all-to-all-start.3 = ((bf16[128,8,160]{0,2,1:T(8,128)(2,1)}), bf16[128,8,160]{0,2,1:T(8,128)(2,1)S(1)}, u32[]{:S(2)}, u32[]{:S(2)}) async-start(bf16[128,8,160]{0,2,1:T(8,128)(2,1)} %copy.63), calls=%async_computation.3 | async-start | bytes 655360 | tf_op jit(solution)/shard_map/all_to_all | solution.py:139
  107.5 64.6 %all_gather.16 = bf16[1280,3,128]{2,0,1:T(8,128)(2,1)S(1)} all-gather(bf16[40,3,128]{2,0,1:T(8,128)(2,1)S(1)} %copy-done.8), channel_id=1, replica_groups=mesh['dp'=32,'head_0'=4,'head_1'=2] {'dp'}, dimensions={0}, use_global_device_ids=true | all-gather | bytes 1013760 | tf_op jit(solution)/shard_map/all_gather | solution.py:122
  172.9 2.6 convert_reduce_fusion.1
  175.8 0.9 fusion.22
  176.7 1.8 fusion.41
  179.1 1.5 copy.62
  180.9 2.4 fusion.50
  183.4 8.4 %while.10 = (s32[]{:T(128)}, bf16[2,1280,64]{1,2,0:T(8,128)(2,1)}, bf16[2,1280,64]{2,1,0:T(8,128)(2,1)S(1)}, bf16[2,1280,64]{2,1,0:T(8,128)(2,1)S(1)}, bf16[2,1280,64]{2,1,0:T(8,128)(2,1)}, /*index=5*/s32[]{:T(128)}) while((s32[]{:T(128)}, bf16[2,1280,64]{1,2,0:T(8,128)(2,1)}, bf16[2,1280,64]{2,1,0:T(8,128)(2,1)S(1)}, ...), condition=%wide.region_7.8_spmd, body=%wide.region_4.7_spmd.sunk | while | flops 429340160 | bytes 24773784 | solution.py:61
  183.4 1.0 fusion.97
  184.4 1.0 fusion.98
  185.6 1.3 fusion.99
  186.8 0.7 copy-done.6
  187.6 1.0 fusion.97
  188.6 1.0 fusion.98
  189.8 1.3 fusion.99
  191.0 0.7 copy-done.6
  191.8 2.6 broadcast_in_dim.36
  194.4 8.3 %all-to-all-start.2 = ((bf16[8,1280,128]{1,2,0:T(8,128)(2,1)}), bf16[8,1280,128]{1,2,0:T(8,128)(2,1)S(1)}, u32[]{:S(2)}, u32[]{:S(2)}) async-start(bf16[8,1280,128]{1,2,0:T(8,128)(2,1)} %broadcast_in_dim.36), calls=%async_computation.2 | async-start | bytes 5242880 | tf_op jit(solution)/shard_map/all_to_all | solution.py:21
  203.3 0.9 copy.64
  204.2 61.5 %all-to-all-done.2 = bf16[8,1280,128]{1,2,0:T(8,128)(2,1)S(1)} async-done(((bf16[8,1280,128]{1,2,0:T(8,128)(2,1)}), bf16[8,1280,128]{1,2,0:T(8,128)(2,1)S(1)}, u32[]{:S(2)}, u32[]{:S(2)}) %all-to-all-start.2) | async-done | bytes 2621472 | tf_op jit(solution)/shard_map/all_to_all | solution.py:21
  265.7 2.3 fusion.46
  268.0 1.4 broadcast_in_dim.37
  269.4 12.6 %all-to-all-start.4 = ((bf16[32,40,640]{2,1,0:T(8,128)(2,1)}), bf16[32,40,640]{2,1,0:T(8,128)(2,1)}, u32[]{:S(2)}, u32[]{:S(2)}) async-start(bf16[32,40,640]{2,1,0:T(8,128)(2,1)} %broadcast_in_dim.37), calls=%async_computation.4 | async-start | bytes 3276800 | tf_op jit(solution)/shard_map/all_to_all | solution.py:21
  282.1 31.7 %all-gather.10.cloned.1.call-done = bf16[32,20,1280]{2,1,0:T(8,128)(2,1)} async-done(((bf16[1,20,1280]{2,1,0:T(8,128)(2,1)}), bf16[32,20,1280]{2,1,0:T(8,128)(2,1)}) %all-gather.10.cloned.1.call-update) | async-done | bytes 1638416 | tf_op jit(solution)/shard_map/all_gather | solution.py:151
  313.8 4.1 reshape.150
  317.9 93.8 %all-gather.8.cloned.1.call-done = bf16[1280,1280]{0,1:T(8,128)(2,1)} async-done(((bf16[1280,160]{0,1:T(8,128)(2,1)}), bf16[1280,1280]{0,1:T(8,128)(2,1)}) %all-gather.8.cloned.1.call-update) | async-done | bytes 3276816 | tf_op jit(solution)/shard_map/all_gather | solution.py:45
  411.8 2.6 convert_reduce_fusion
  414.7 0.9 fusion.18
  415.6 15.6 %convolution_convert_fusion = bf16[1280,1280]{0,1:T(8,128)(2,1)} fusion(bf16[640,1280]{1,0:T(8,128)(2,1)} %reshape.150, bf16[1280,640]{1,0:T(8,128)(2,1)} %bitcast.24, bf16[1280,1280]{0,1:T(8,128)(2,1)S(1)} %copy-done.1, f32[1280]{0:T(1024)S(1)} %copy-done.15, f32[1280]{0:T(1024)S(1)} %copy-done.16, f32[1280]{0:T(1024)S(1)} %add_rsqrt_fusion, ...), kind=kOutput, calls=%fused_computation.25 | convolution fusion | flops 4259840000 | bytes 9853440 | tf_op jit(solution)/shard_map/dot_general | solution.py:89
  431.2 4.0 copy.71
  435.3 37.3 %reduce-scatter.3.cloned.1.call-done = bf16[2560,160]{0,1:T(8,128)(2,1)} async-done(((bf16[10240,160]{0,1:T(8,128)(2,1)}), bf16[2560,160]{0,1:T(8,128)(2,1)}) %reduce-scatter.3.cloned.1.call-update) | async-done | bytes 819216 | tf_op jit(solution)/shard_map/reduce_scatter | solution.py:31
  472.7 35.9 %reduce-scatter.5.cloned.1.call-done = bf16[1280,160]{0,1:T(8,128)(2,1)} async-done(((bf16[2560,160]{0,1:T(8,128)(2,1)}), bf16[1280,160]{0,1:T(8,128)(2,1)}) %reduce-scatter.5.cloned.1.call-update) | async-done | bytes 409616 | tf_op jit(solution)/shard_map/reduce_scatter | solution.py:31
  508.6 1.2 add_convert_fusion.1
  510.0 1.6 reshape.138
  (80 shorter events, 5.6 us)
Async XLA Ops:
  7.4 16.0 %copy-start.18 = (s32[32]{0:T(128)S(1)}, s32[32]{0:T(128)}, u32[]{:S(2)}) copy-start(s32[32]{0:T(128)} %param.29) | copy-start | bytes 388
  14.3 20.7 %all-to-all-start = ((bf16[32,2,3200]{2,1,0:T(2,128)(2,1)}), bf16[32,2,3200]{2,1,0:T(2,128)(2,1)S(1)}, u32[]{:S(2)}, u32[]{:S(2)}) async-start(bf16[32,2,3200]{2,1,0:T(2,128)(2,1)} %reshape.166), calls=%async_computation | async-start | bytes 819200 | tf_op jit(solution)/shard_map/all_to_all | solution.py:81
  23.3 149.6 %all-gather.6.cloned.1.call-start = ((), (), s32[]{:S(2)}) async-start(), calls=%async_computation.7 | async-start | bytes 3686400 | tf_op jit(solution)/shard_map/all_gather | solution.py:45
  37.1 22.6 %copy-start.9 = (bf16[4,1280]{1,0:T(4,128)(2,1)S(1)}, bf16[4,1280]{1,0:T(4,128)(2,1)}, u32[]{:S(2)}) copy-start(bf16[4,1280]{1,0:T(4,128)(2,1)} %param.21) | copy-start | bytes 30724
  55.4 52.1 %copy-start.8 = (bf16[40,3,128]{2,0,1:T(8,128)(2,1)S(1)}, bf16[40,3,128]{2,0,1:T(8,128)(2,1)}, u32[]{:S(2)}) copy-start(bf16[40,3,128]{2,0,1:T(8,128)(2,1)} %param.19) | copy-start | bytes 92164
  59.7 113.0 %copy-start.10 = (f32[2,128]{1,0:T(2,128)S(1)}, f32[2,128]{1,0:T(2,128)}, u32[]{:S(2)}) copy-start(f32[2,128]{1,0:T(2,128)} %param.20) | copy-start | bytes 3076
  100.3 91.5 %all-to-all-start.3 = ((bf16[128,8,160]{0,2,1:T(8,128)(2,1)}), bf16[128,8,160]{0,2,1:T(8,128)(2,1)S(1)}, u32[]{:S(2)}, u32[]{:S(2)}) async-start(bf16[128,8,160]{0,2,1:T(8,128)(2,1)} %copy.63), calls=%async_computation.3 | async-start | bytes 655360 | tf_op jit(solution)/shard_map/all_to_all | solution.py:139
  172.9 3.9 copy-start.13
  172.9 3.9 copy-start.14
  172.9 2.9 copy-start
  184.4 1.1 copy-start.4
  184.4 1.2 copy-start.5
  186.8 0.7 copy-start.6
  188.6 1.1 copy-start.4
  188.6 1.2 copy-start.5
  191.0 0.7 copy-start.6
  194.4 71.2 %copy-start.2 = (bf16[1280,160]{0,1:T(8,128)(2,1)S(1)}, bf16[1280,160]{0,1:T(8,128)(2,1)}, u32[]{:S(2)}) copy-start(bf16[1280,160]{0,1:T(8,128)(2,1)} %copy.56) | copy-start | bytes 1228804
  194.4 71.2 %copy-start.12 = (f32[160]{0:T(256)S(1)}, f32[160]{0:T(256)}, u32[]{:S(2)}) copy-start(f32[160]{0:T(256)} %param.22) | copy-start | bytes 1924
  194.4 71.2 %all-to-all-start.2 = ((bf16[8,1280,128]{1,2,0:T(8,128)(2,1)}), bf16[8,1280,128]{1,2,0:T(8,128)(2,1)S(1)}, u32[]{:S(2)}, u32[]{:S(2)}) async-start(bf16[8,1280,128]{1,2,0:T(8,128)(2,1)} %broadcast_in_dim.36), calls=%async_computation.2 | async-start | bytes 5242880 | tf_op jit(solution)/shard_map/all_to_all | solution.py:21
  202.7 65.3 %copy-start.7 = (bf16[40,640]{1,0:T(8,128)(2,1)S(1)}, bf16[40,640]{1,0:T(8,128)(2,1)}, u32[]{:S(2)}) copy-start(bf16[40,640]{1,0:T(8,128)(2,1)} %param.25) | copy-start | bytes 153604
  202.7 111.1 %all-gather.10.cloned.1.call-start = ((), (), s32[]{:S(2)}) async-start(), calls=%async_computation.11 | async-start | bytes 2027520 | tf_op jit(solution)/shard_map/all_gather | solution.py:151
  203.3 208.5 %all-gather.8.cloned.1.call-start = ((), (), s32[]{:S(2)}) async-start(), calls=%async_computation.8 | async-start | bytes 3686400 | tf_op jit(solution)/shard_map/all_gather | solution.py:45
  269.4 146.2 %all-to-all-start.4 = ((bf16[32,40,640]{2,1,0:T(8,128)(2,1)}), bf16[32,40,640]{2,1,0:T(8,128)(2,1)}, u32[]{:S(2)}, u32[]{:S(2)}) async-start(bf16[32,40,640]{2,1,0:T(8,128)(2,1)} %broadcast_in_dim.37), calls=%async_computation.4 | async-start | bytes 3276800 | tf_op jit(solution)/shard_map/all_to_all | solution.py:21
  282.0 190.6 %reduce-scatter.3.cloned.1.call-start = ((), (), s32[]{:S(2)}) async-start(), calls=%async_computation.9 | async-start | bytes 4096000 | tf_op jit(solution)/shard_map/reduce_scatter | solution.py:31
  317.9 97.7 %copy-start.15 = (f32[1280]{0:T(1024)S(1)}, f32[1280]{0:T(1024)}, u32[]{:S(2)}) copy-start(f32[1280]{0:T(1024)} %param.24) | copy-start | bytes 15364
  317.9 97.7 %copy-start.16 = (f32[1280]{0:T(1024)S(1)}, f32[1280]{0:T(1024)}, u32[]{:S(2)}) copy-start(f32[1280]{0:T(1024)} %param.23) | copy-start | bytes 15364
  317.9 97.7 %copy-start.17 = (f32[640]{0:T(1024)S(1)}, f32[640]{0:T(1024)}, u32[]{:S(2)}) copy-start(f32[640]{0:T(1024)} %param.26) | copy-start | bytes 7684
  411.8 2.9 copy-start.1
  435.2 73.3 %copy-start.3 = (bf16[1280,160]{0,1:T(8,128)(2,1)S(1)}, bf16[1280,160]{0,1:T(8,128)(2,1)}, u32[]{:S(2)}) copy-start(bf16[1280,160]{0,1:T(8,128)(2,1)} %fusion.46) | copy-start | bytes 1228804
  435.2 73.3 %copy-start.11 = (f32[160]{0:T(256)S(1)}, f32[160]{0:T(256)}, u32[]{:S(2)}) copy-start(f32[160]{0:T(256)} %param.28) | copy-start | bytes 1924
  435.3 73.3 %reduce-scatter.5.cloned.1.call-start = ((), (), s32[]{:S(2)}) async-start(), calls=%async_computation.10 | async-start | bytes 1228800 | tf_op jit(solution)/shard_map/reduce_scatter | solution.py:31
Sparse Core Ops, SparseCore 0:
  59.8 99.7 all-gather.5
  435.4 37.2 reduce-scatter.2
Sparse Core Ops, SparseCore 1:
  205.1 108.7 all-gather.9
  316.3 95.4 all-gather.7
  472.8 35.7 reduce-scatter.4
where the time goes:
time: 528 us; the launch traced here: 519 us
  waiting for transfers between devices  272 us (52%)
  blocking collectives  121 us (23%)
  starting transfers between devices  37.3 us (7%)
  local copies, waits for them, and re-layouts  29.5 us (6%)
  matrix products  24.3 us (5%)
  other arithmetic  19.4 us (4%)
  between operations  15.5 us (3%)
    all_gather x2, waiting for transfers between devices, normalize(): whole_rows = lax.all_gather(residual_in, HEAD, axis=1, tiled=True)  93.8 us
    reduce_scatter x2, waiting for transfers between devices, own_rows(): total = lax.psum_scatter(total, axis, scatter_dimension=0, tiled=True)  73.2 us
    all_gather x1, blocking collectives, on_device(): weight_piece = lax.all_gather(qkv_weight, 'dp', axis=0, tiled=True)  64.6 us
    all_to_all x2, waiting for transfers between devices, sent_to_all(): return lax.all_to_all(copies, axis, split_axis=0, concat_axis=0, tiled=True)  61.5 us
    all_gather x1, blocking collectives, on_device(): output_rows = lax.all_gather(out_weight, 'dp', axis=0, tiled=True)  38.8 us
    all_gather x1, waiting for transfers between devices, on_device(): down_rows = lax.all_gather(fc2_weight, 'dp', axis=0, tiled=True)  31.7 us
    all_to_all x2, starting transfers between devices, sent_to_all(): return lax.all_to_all(copies, axis, split_axis=0, concat_axis=0, tiled=True)  20.9 us
    all_to_all x1, blocking collectives, regroup(): lax.all_to_all(picked, 'dp', split_axis=0, concat_axis=0, tiled=True)  17.8 us
  transfers between devices with their start and end apart: 9, of which 6 were waited for; matrix products, arithmetic and copies ran while one was open for 6% of the time, Pallas kernels for 0%

commit v1 on v0

--- a/solution.py
+++ b/solution.py
@@ -132,7 +132,9 @@
     key_rows = projected[:, 1].astype(jnp.bfloat16).reshape(frame_count, -1, HDIM)
     value_rows = (projected[:, 2] + qv_bias[1]).astype(jnp.bfloat16).reshape(frame_count, -1, HDIM)
     context = attend(queries, key_rows, value_rows)
-    output_rows = lax.all_gather(out_weight, "dp", axis=0, tiled=True)
+    output_rows = jnp.concatenate(
+        lax.all_to_all(jnp.stack([out_weight] * lax.axis_size("dp")), "dp", 0, 0), axis=0
+    )
     carried = residual_in.astype(jnp.float32) + out_bias
     whole_context = gather_directly(context, HEAD, 1)
     split_rows = output_rows.reshape(output_rows.shape[0], head_count, local_width)

time: 528 us -> 512 us (0.970)
  blocking collectives: 121 us -> 67.6 us
  starting transfers between devices: 37.3 us -> 79.9 us
  waiting for transfers between devices: 272 us -> 266 us
    all_gather x1 -> x0, blocking collectives: 38.8 us -> none  [on_device(): output_rows = lax.all_gather(out_weight, 'dp', axis=0, tiled=True)]
    all_gather x2, waiting for transfers between devices: 93.8 us -> 124 us  [normalize(): whole_rows = lax.all_gather(residual_in, HEAD, axis=1, tiled=True)]
    all_to_all x2, waiting for transfers between devices: 61.5 us -> 32.6 us  [sent_to_all(): return lax.all_to_all(copies, axis, split_axis=0, concat_axis=0, tiled=True)]
    all_to_all x2, starting transfers between devices: 20.9 us -> 46.1 us  [sent_to_all(): return lax.all_to_all(copies, axis, split_axis=0, concat_axis=0, tiled=True)]
    all_gather x1, blocking collectives: 64.6 us -> 49.8 us  [on_device(): weight_piece = lax.all_gather(qkv_weight, 'dp', axis=0, tiled=True)]
    all_to_all x1, starting transfers between devices: 7.22 us -> 18.1 us  [on_device(): lax.all_to_all(split_rows, HEAD, split_axis=1, concat_axis=0, tiled=True)]
    all_gather x1, waiting for transfers between devices: 31.7 us -> 23.9 us  [on_device(): down_rows = lax.all_gather(fc2_weight, 'dp', axis=0, tiled=True)]
    all_to_all x0 -> x1, starting transfers between devices: none -> 6.39 us  [on_device(): lax.all_to_all(jnp.stack([out_weight] * lax.axis_size('dp')), 'dp', 0, 0)]
  transfers between devices with their start and end apart: 9 -> 10, of which waited for: 6 -> 7; matrix products, arithmetic and copies ran while one was open for 6% -> 6% of each run, Pallas kernels for 0% -> 0%
where the time goes in v1:
time: 512 us; the launch traced here: 503 us
  waiting for transfers between devices  266 us (52%)
  starting transfers between devices  79.9 us (16%)
  blocking collectives  67.6 us (13%)
  local copies, waits for them, and re-layouts  29.9 us (6%)
  matrix products  24.4 us (5%)
  other arithmetic  19.3 us (4%)
  between operations  15.7 us (3%)
    all_gather x2, waiting for transfers between devices, normalize(): whole_rows = lax.all_gather(residual_in, HEAD, axis=1, tiled=True)  124 us
    reduce_scatter x2, waiting for transfers between devices, own_rows(): total = lax.psum_scatter(total, axis, scatter_dimension=0, tiled=True)  73.2 us
    all_gather x1, blocking collectives, on_device(): weight_piece = lax.all_gather(qkv_weight, 'dp', axis=0, tiled=True)  49.8 us
    all_to_all x2, starting transfers between devices, sent_to_all(): return lax.all_to_all(copies, axis, split_axis=0, concat_axis=0, tiled=True)  46.1 us
    all_to_all x2, waiting for transfers between devices, sent_to_all(): return lax.all_to_all(copies, axis, split_axis=0, concat_axis=0, tiled=True)  32.6 us
    all_gather x1, waiting for transfers between devices, on_device(): down_rows = lax.all_gather(fc2_weight, 'dp', axis=0, tiled=True)  23.9 us
    all_to_all x1, starting transfers between devices, on_device(): lax.all_to_all(split_rows, HEAD, split_axis=1, concat_axis=0, tiled=True)  18.1 us
    all_to_all x1, blocking collectives, regroup(): lax.all_to_all(picked, 'dp', split_axis=0, concat_axis=0, tiled=True)  17.8 us
  transfers between devices with their start and end apart: 10, of which 7 were waited for; matrix products, arithmetic and copies ran while one was open for 6% of the time, Pallas kernels for 0%

profile of v1, /device:TPU:2, one launch (start us, length us, event | category | flops | bytes accessed | tf_op | source)
XLA Modules:
  0.0 502.7 jit_solution(14783118371410706284)
XLA Ops:
  7.4 2.4 all_to_all.42
  10.3 3.0 reduce.9
  13.3 0.9 reshape.161
  14.2 9.1 %all-to-all-start = ((bf16[32,2,3200]{2,1,0:T(2,128)(2,1)}), bf16[32,2,3200]{2,1,0:T(2,128)(2,1)S(1)}, u32[]{:S(2)}, u32[]{:S(2)}) async-start(bf16[32,2,3200]{2,1,0:T(2,128)(2,1)} %reshape.161), calls=%async_computation | async-start | bytes 819200 | tf_op jit(solution)/shard_map/all_to_all | solution.py:81
  23.6 11.2 %all-to-all-done = bf16[32,2,3200]{2,1,0:T(2,128)(2,1)S(1)} async-done(((bf16[32,2,3200]{2,1,0:T(2,128)(2,1)}), bf16[32,2,3200]{2,1,0:T(2,128)(2,1)S(1)}, u32[]{:S(2)}, u32[]{:S(2)}) %all-to-all-start) | async-done | bytes 409632 | tf_op jit(solution)/shard_map/all_to_all | solution.py:81
  35.3 0.8 gather_fusion
  36.2 0.9 reduce.10
  37.2 17.8 %all_to_all.49 = bf16[32,2,3200]{2,1,0:T(2,128)(2,1)S(1)} all-to-all(bf16[32,2,3200]{2,1,0:T(2,128)(2,1)S(1)} %reshape.163), channel_id=1, replica_groups=mesh['dp'=32,'head_0'=4,'head_1'=2] {'dp'}, dimensions={0} | all-to-all | bytes 819200 | tf_op jit(solution)/shard_map/all_to_all | solution.py:83
  55.3 2.4 reduce
  57.8 0.8 reshape.130
  58.6 1.0 copy.56
  59.6 0.8 stack.2
  60.4 6.4 %all-to-all-start.3 = ((bf16[32,4,1280]{2,1,0:T(4,128)(2,1)}), bf16[32,4,1280]{2,1,0:T(4,128)(2,1)S(1)}, u32[]{:S(2)}, u32[]{:S(2)}) async-start(bf16[32,4,1280]{2,1,0:T(4,128)(2,1)} %stack.2), calls=%async_computation.3 | async-start | bytes 655360 | tf_op jit(solution)/shard_map/all_to_all | solution.py:136
  66.9 49.8 %all_gather.13 = bf16[1280,3,128]{2,0,1:T(8,128)(2,1)S(1)} all-gather(bf16[40,3,128]{2,0,1:T(8,128)(2,1)S(1)} %copy-done.8), channel_id=1, replica_groups=mesh['dp'=32,'head_0'=4,'head_1'=2] {'dp'}, dimensions={0}, use_global_device_ids=true | all-gather | bytes 1013760 | tf_op jit(solution)/shard_map/all_gather | solution.py:122
  118.1 1.1 copy.63
  119.2 18.1 %all-to-all-start.4 = ((bf16[128,8,160]{0,2,1:T(8,128)(2,1)}), bf16[128,8,160]{0,2,1:T(8,128)(2,1)S(1)}, u32[]{:S(2)}, u32[]{:S(2)}) async-start(bf16[128,8,160]{0,2,1:T(8,128)(2,1)} %copy.63), calls=%async_computation.4 | async-start | bytes 655360 | tf_op jit(solution)/shard_map/all_to_all | solution.py:141
  137.3 20.6 %all-gather.5.cloned.1.call-done = bf16[1280,1280]{0,1:T(8,128)(2,1)} async-done(((bf16[1280,160]{0,1:T(8,128)(2,1)}), bf16[1280,1280]{0,1:T(8,128)(2,1)}) %all-gather.5.cloned.1.call-update) | async-done | bytes 3276816 | tf_op jit(solution)/shard_map/all_gather | solution.py:45
  157.9 2.6 convert_reduce_fusion.1
  160.8 0.9 fusion.22
  161.7 1.8 fusion.41
  164.1 1.5 copy.62
  165.9 2.4 fusion.50
  168.3 8.4 %while.10 = (s32[]{:T(128)}, bf16[2,1280,64]{1,2,0:T(8,128)(2,1)}, bf16[2,1280,64]{2,1,0:T(8,128)(2,1)S(1)}, bf16[2,1280,64]{2,1,0:T(8,128)(2,1)S(1)}, bf16[2,1280,64]{2,1,0:T(8,128)(2,1)}, /*index=5*/s32[]{:T(128)}) while((s32[]{:T(128)}, bf16[2,1280,64]{1,2,0:T(8,128)(2,1)}, bf16[2,1280,64]{2,1,0:T(8,128)(2,1)S(1)}, ...), condition=%wide.region_7.8_spmd, body=%wide.region_4.7_spmd.sunk | while | flops 429340160 | bytes 24773784 | solution.py:61
  168.3 1.0 fusion.97
  169.4 1.0 fusion.98
  170.5 1.3 fusion.99
  171.8 0.7 copy-done.6
  172.5 1.0 fusion.97
  173.6 1.0 fusion.98
  174.7 1.3 fusion.99
  176.7 2.6 broadcast_in_dim.36
  179.4 3.8 all-to-all-start.2
  183.8 0.9 copy.64
  184.6 32.6 %all-to-all-done.2 = bf16[8,1280,128]{1,2,0:T(8,128)(2,1)S(1)} async-done(((bf16[8,1280,128]{1,2,0:T(8,128)(2,1)}), bf16[8,1280,128]{1,2,0:T(8,128)(2,1)S(1)}, u32[]{:S(2)}, u32[]{:S(2)}) %all-to-all-start.2) | async-done | bytes 2621472 | tf_op jit(solution)/shard_map/all_to_all | solution.py:21
  217.2 2.3 fusion.46
  219.6 1.3 broadcast_in_dim.37
  221.0 42.4 %all-to-all-start.5 = ((bf16[32,40,640]{2,1,0:T(8,128)(2,1)}), bf16[32,40,640]{2,1,0:T(8,128)(2,1)}, u32[]{:S(2)}, u32[]{:S(2)}) async-start(bf16[32,40,640]{2,1,0:T(8,128)(2,1)} %broadcast_in_dim.37), calls=%async_computation.5 | async-start | bytes 3276800 | tf_op jit(solution)/shard_map/all_to_all | solution.py:21
  263.4 23.9 %all-gather.9.cloned.1.call-done = bf16[32,20,1280]{2,1,0:T(8,128)(2,1)} async-done(((bf16[1,20,1280]{2,1,0:T(8,128)(2,1)}), bf16[32,20,1280]{2,1,0:T(8,128)(2,1)}) %all-gather.9.cloned.1.call-update) | async-done | bytes 1638416 | tf_op jit(solution)/shard_map/all_gather | solution.py:153
  287.3 3.8 reshape.146
  291.2 103.8 %all-gather.7.cloned.1.call-done = bf16[1280,1280]{0,1:T(8,128)(2,1)} async-done(((bf16[1280,160]{0,1:T(8,128)(2,1)}), bf16[1280,1280]{0,1:T(8,128)(2,1)}) %all-gather.7.cloned.1.call-update) | async-done | bytes 3276816 | tf_op jit(solution)/shard_map/all_gather | solution.py:45
  394.9 2.6 convert_reduce_fusion
  397.8 0.9 fusion.18
  398.8 15.6 %convolution_convert_fusion = bf16[1280,1280]{0,1:T(8,128)(2,1)} fusion(bf16[640,1280]{1,0:T(8,128)(2,1)} %reshape.146, bf16[1280,640]{1,0:T(8,128)(2,1)} %bitcast.23, bf16[1280,1280]{0,1:T(8,128)(2,1)S(1)} %copy-done.1, f32[1280]{0:T(1024)S(1)} %copy-done.15, f32[1280]{0:T(1024)S(1)} %copy-done.16, f32[1280]{0:T(1024)S(1)} %add_rsqrt_fusion, ...), kind=kOutput, calls=%fused_computation.25 | convolution fusion | flops 4259840000 | bytes 9853440 | tf_op jit(solution)/shard_map/dot_general | solution.py:89
  414.4 4.0 copy.71
  418.5 37.3 %reduce-scatter.3.cloned.1.call-done = bf16[2560,160]{0,1:T(8,128)(2,1)} async-done(((bf16[10240,160]{0,1:T(8,128)(2,1)}), bf16[2560,160]{0,1:T(8,128)(2,1)}) %reduce-scatter.3.cloned.1.call-update) | async-done | bytes 819216 | tf_op jit(solution)/shard_map/reduce_scatter | solution.py:31
  455.9 35.9 %reduce-scatter.5.cloned.1.call-done = bf16[1280,160]{0,1:T(8,128)(2,1)} async-done(((bf16[2560,160]{0,1:T(8,128)(2,1)}), bf16[1280,160]{0,1:T(8,128)(2,1)}) %reduce-scatter.5.cloned.1.call-update) | async-done | bytes 409616 | tf_op jit(solution)/shard_map/reduce_scatter | solution.py:31
  491.8 1.2 add_convert_fusion.1
  493.2 1.6 reshape.136
  (82 shorter events, 6.9 us)
Async XLA Ops:
  7.4 15.9 %copy-start.18 = (s32[32]{0:T(128)S(1)}, s32[32]{0:T(128)}, u32[]{:S(2)}) copy-start(s32[32]{0:T(128)} %param.29) | copy-start | bytes 388
  14.2 20.7 %all-to-all-start = ((bf16[32,2,3200]{2,1,0:T(2,128)(2,1)}), bf16[32,2,3200]{2,1,0:T(2,128)(2,1)S(1)}, u32[]{:S(2)}, u32[]{:S(2)}) async-start(bf16[32,2,3200]{2,1,0:T(2,128)(2,1)} %reshape.161), calls=%async_computation | async-start | bytes 819200 | tf_op jit(solution)/shard_map/all_to_all | solution.py:81
  23.2 134.7 %all-gather.5.cloned.1.call-start = ((), (), s32[]{:S(2)}) async-start(), calls=%async_computation.8 | async-start | bytes 3686400 | tf_op jit(solution)/shard_map/all_gather | solution.py:45
  37.0 22.6 %copy-start.9 = (bf16[4,1280]{1,0:T(4,128)(2,1)S(1)}, bf16[4,1280]{1,0:T(4,128)(2,1)}, u32[]{:S(2)}) copy-start(bf16[4,1280]{1,0:T(4,128)(2,1)} %param.21) | copy-start | bytes 30724
  37.2 29.7 %copy-start.8 = (bf16[40,3,128]{2,0,1:T(8,128)(2,1)S(1)}, bf16[40,3,128]{2,0,1:T(8,128)(2,1)}, u32[]{:S(2)}) copy-start(bf16[40,3,128]{2,0,1:T(8,128)(2,1)} %param.19) | copy-start | bytes 92164
  57.8 59.5 %copy-start.10 = (f32[2,128]{1,0:T(2,128)S(1)}, f32[2,128]{1,0:T(2,128)}, u32[]{:S(2)}) copy-start(f32[2,128]{1,0:T(2,128)} %param.20) | copy-start | bytes 3076
  60.4 57.0 %all-to-all-start.3 = ((bf16[32,4,1280]{2,1,0:T(4,128)(2,1)}), bf16[32,4,1280]{2,1,0:T(4,128)(2,1)S(1)}, u32[]{:S(2)}, u32[]{:S(2)}) async-start(bf16[32,4,1280]{2,1,0:T(4,128)(2,1)} %stack.2), calls=%async_computation.3 | async-start | bytes 655360 | tf_op jit(solution)/shard_map/all_to_all | solution.py:136
  119.2 57.5 %all-to-all-start.4 = ((bf16[128,8,160]{0,2,1:T(8,128)(2,1)}), bf16[128,8,160]{0,2,1:T(8,128)(2,1)S(1)}, u32[]{:S(2)}, u32[]{:S(2)}) async-start(bf16[128,8,160]{0,2,1:T(8,128)(2,1)} %copy.63), calls=%async_computation.4 | async-start | bytes 655360 | tf_op jit(solution)/shard_map/all_to_all | solution.py:141
  137.3 24.4 %copy-start.13 = (f32[1280]{0:T(1024)S(1)}, f32[1280]{0:T(1024)}, u32[]{:S(2)}) copy-start(f32[1280]{0:T(1024)} %param.18) | copy-start | bytes 15364
  137.3 24.4 %copy-start.14 = (f32[1280]{0:T(1024)S(1)}, f32[1280]{0:T(1024)}, u32[]{:S(2)}) copy-start(f32[1280]{0:T(1024)} %param.17) | copy-start | bytes 15364
  157.9 2.9 copy-start
  169.4 1.1 copy-start.4
  169.4 1.2 copy-start.5
  171.8 0.7 copy-start.6
  173.6 1.1 copy-start.4
  173.6 1.2 copy-start.5
  176.0 0.7 copy-start.6
  179.3 37.9 %copy-start.2 = (bf16[1280,160]{0,1:T(8,128)(2,1)S(1)}, bf16[1280,160]{0,1:T(8,128)(2,1)}, u32[]{:S(2)}) copy-start(bf16[1280,160]{0,1:T(8,128)(2,1)} %copy.56) | copy-start | bytes 1228804
  179.4 37.9 %copy-start.12 = (f32[160]{0:T(256)S(1)}, f32[160]{0:T(256)}, u32[]{:S(2)}) copy-start(f32[160]{0:T(256)} %param.22) | copy-start | bytes 1924
  179.4 37.9 %all-to-all-start.2 = ((bf16[8,1280,128]{1,2,0:T(8,128)(2,1)}), bf16[8,1280,128]{1,2,0:T(8,128)(2,1)S(1)}, u32[]{:S(2)}, u32[]{:S(2)}) async-start(bf16[8,1280,128]{1,2,0:T(8,128)(2,1)} %broadcast_in_dim.36), calls=%async_computation.2 | async-start | bytes 5242880 | tf_op jit(solution)/shard_map/all_to_all | solution.py:21
  183.1 36.5 %copy-start.7 = (bf16[40,640]{1,0:T(8,128)(2,1)S(1)}, bf16[40,640]{1,0:T(8,128)(2,1)}, u32[]{:S(2)}) copy-start(bf16[40,640]{1,0:T(8,128)(2,1)} %param.25) | copy-start | bytes 153604
  183.1 104.2 %all-gather.9.cloned.1.call-start = ((), (), s32[]{:S(2)}) async-start(), calls=%async_computation.12 | async-start | bytes 2027520 | tf_op jit(solution)/shard_map/all_gather | solution.py:153
  183.7 211.2 %all-gather.7.cloned.1.call-start = ((), (), s32[]{:S(2)}) async-start(), calls=%async_computation.9 | async-start | bytes 3686400 | tf_op jit(solution)/shard_map/all_gather | solution.py:45
  221.0 177.8 %all-to-all-start.5 = ((bf16[32,40,640]{2,1,0:T(8,128)(2,1)}), bf16[32,40,640]{2,1,0:T(8,128)(2,1)}, u32[]{:S(2)}, u32[]{:S(2)}) async-start(bf16[32,40,640]{2,1,0:T(8,128)(2,1)} %broadcast_in_dim.37), calls=%async_computation.5 | async-start | bytes 3276800 | tf_op jit(solution)/shard_map/all_to_all | solution.py:21
  263.3 192.5 %reduce-scatter.3.cloned.1.call-start = ((), (), s32[]{:S(2)}) async-start(), calls=%async_computation.10 | async-start | bytes 4096000 | tf_op jit(solution)/shard_map/reduce_scatter | solution.py:31
  291.1 107.6 %copy-start.15 = (f32[1280]{0:T(1024)S(1)}, f32[1280]{0:T(1024)}, u32[]{:S(2)}) copy-start(f32[1280]{0:T(1024)} %param.24) | copy-start | bytes 15364
  291.1 107.6 %copy-start.16 = (f32[1280]{0:T(1024)S(1)}, f32[1280]{0:T(1024)}, u32[]{:S(2)}) copy-start(f32[1280]{0:T(1024)} %param.23) | copy-start | bytes 15364
  291.1 107.6 %copy-start.17 = (f32[640]{0:T(1024)S(1)}, f32[640]{0:T(1024)}, u32[]{:S(2)}) copy-start(f32[640]{0:T(1024)} %param.26) | copy-start | bytes 7684
  394.9 2.9 copy-start.1
  418.4 73.3 %copy-start.3 = (bf16[1280,160]{0,1:T(8,128)(2,1)S(1)}, bf16[1280,160]{0,1:T(8,128)(2,1)}, u32[]{:S(2)}) copy-start(bf16[1280,160]{0,1:T(8,128)(2,1)} %fusion.46) | copy-start | bytes 1228804
  418.4 73.3 %copy-start.11 = (f32[160]{0:T(256)S(1)}, f32[160]{0:T(256)}, u32[]{:S(2)}) copy-start(f32[160]{0:T(256)} %param.28) | copy-start | bytes 1924
  418.5 73.3 %reduce-scatter.5.cloned.1.call-start = ((), (), s32[]{:S(2)}) async-start(), calls=%async_computation.11 | async-start | bytes 1228800 | tf_op jit(solution)/shard_map/reduce_scatter | solution.py:31
Sparse Core Ops, SparseCore 0:
  59.7 98.1 all-gather.4
  418.6 37.2 reduce-scatter.2
Sparse Core Ops, SparseCore 1:
  185.5 101.8 all-gather.8
  289.8 105.0 all-gather.6
  456.0 35.7 reduce-scatter.4
